TPU v7x, 8 devices: a whole 2x2x1 slice. The times are simulated.
8 devices in a mesh: col: 4 (over z, y, x), row: 2 (over core).
Axes of the slice: x: 2, y: 2, z: 1, core: 2. Of those that a mesh axis runs over, the one named last changes fastest.
Arguments:
- vel_u: float32 [31, 512, 2048], P(None, 'row', 'col')
- vel_v: float32 [31, 512, 2048], P(None, 'row', 'col')
- temperature: float32 [31, 512, 2048], P(None, 'row', 'col')
- salinity: float32 [31, 512, 2048], P(None, 'row', 'col')
- sea_level: float32 [512, 2048], P('row', 'col')
- trans_u: float32 [512, 2048], P('row', 'col')
- trans_v: float32 [512, 2048], P('row', 'col')
- bathymetry: float32 [512, 2048], P('row', 'col')
- kmt_levels: int32 [512, 2048], P('row', 'col')
- tide_force: float32 [30, 2], replicated
Outputs:
- output 1: float32 [512, 2048], P('row', 'col')
- output 2: float32 [512, 2048], P('row', 'col')
- output 3: float32 [512, 2048], P('row', 'col')
- output 4: float32 [31, 512, 2048], P(None, 'row', 'col')
- output 5: float32 [31, 512, 2048], P(None, 'row', 'col')
- output 6: float32 [31, 512, 2048], P(None, 'row', 'col')
- output 7: float32 [31, 512, 2048], P(None, 'row', 'col')
All inputs are finite; a program needn't handle non-finite values.
Results may differ from a plain program's by a relative error of at most 0.001.
Values sent between devices are 32-bit elements.
A program may use at most 1 GiB of HBM per device.

v0:
```python
import jax
import jax.numpy as jnp
from jax import lax
from jax.sharding import PartitionSpec as P

GRAVITY = 1.0
GRID_DX = 1.0
TIME_STEP = 4.0
ALPHA_T = 0.02
BETA_S = 0.015
T_REF = 1.0
S_REF = 1.0
VISC_KV = 0.001
DIFF_KT = 0.0005


def level_mask(count, n_levels):
    levels = jnp.arange(n_levels, dtype=jnp.int32)[:, None, None]
    return (levels < count[None]).astype(jnp.float32)


def interface_coef(count, thick, kappa, n_levels):
    levels = jnp.arange(n_levels - 1, dtype=jnp.int32)[:, None, None]
    active = (levels + 1 < count[None]).astype(jnp.float32)
    safe = jnp.where(count > 0, thick, 1.0)
    return active * (TIME_STEP * kappa / (safe * safe))[None]


def column_solve(source, couple):
    edge = jnp.zeros_like(source[:1])
    upper = jnp.concatenate([couple, edge], axis=0)
    lower = jnp.concatenate([edge, couple], axis=0)
    diag = 1.0 + upper + lower

    def forward(carry, slab):
        gain_prev, part_prev = carry
        lower_k, diag_k, upper_k, source_k = slab
        pivot = diag_k - lower_k * gain_prev
        gain = upper_k / pivot
        part = (source_k + lower_k * part_prev) / pivot
        return (gain, part), (gain, part)

    start = (jnp.zeros_like(source[0]), jnp.zeros_like(source[0]))
    _, (gains, parts) = lax.scan(forward, start, (lower, diag, upper, source))

    def backward(below, slab):
        gain, part = slab
        here = part + gain * below
        return here, here

    _, profile = lax.scan(backward, jnp.zeros_like(source[0]), (gains, parts), reverse=True)
    return profile


def geometry(kmt_ext, depth_ext):
    kmt_cell = kmt_ext[1:-1, 1:-1]
    thick_ext = depth_ext / jnp.maximum(kmt_ext, 1).astype(jnp.float32)
    thick_cell = thick_ext[1:-1, 1:-1]
    return {"k_cell": kmt_cell, "k_u": jnp.minimum(kmt_cell, kmt_ext[1:-1, 2:]), "k_v": jnp.minimum(kmt_cell, kmt_ext[2:, 1:-1]), "dz_cell": thick_cell, "dz_u": 0.5 * (thick_cell + thick_ext[1:-1, 2:]), "dz_v": 0.5 * (thick_cell + thick_ext[2:, 1:-1])}


def surface_fields(layout):
    k_faces = jnp.stack([layout["k_u"], layout["k_v"]])
    face_depth = k_faces.astype(jnp.float32) * jnp.stack([layout["dz_u"], layout["dz_v"]])
    face_wet = (k_faces > 0).astype(jnp.float32)
    wet_cell = (layout["k_cell"] > 0).astype(jnp.float32)
    return face_depth, face_wet, wet_cell


def momentum_tend(u_ext, v_ext, p_ext):
    cen_u = 0.5 * (u_ext[:, 1:-1, :-1] + u_ext[:, 1:-1, 1:])
    corner_v = 0.5 * (v_ext[:, :-1, 1:-1] + v_ext[:, :-1, 2:])
    corner_u = 0.5 * (u_ext[:, :-1, 1:-1] + u_ext[:, 1:, 1:-1])
    flux_uu = cen_u * cen_u
    flux_vu = corner_v * corner_u
    tend_u = -(flux_uu[:, :, 1:] - flux_uu[:, :, :-1] + flux_vu[:, 1:, :] - flux_vu[:, :-1, :] + p_ext[:, 1:-1, 2:] - p_ext[:, 1:-1, 1:-1]) / GRID_DX
    cen_v = 0.5 * (v_ext[:, :-1, 1:-1] + v_ext[:, 1:, 1:-1])
    side_u = 0.5 * (u_ext[:, 1:-1, :-1] + u_ext[:, 2:, :-1])
    side_v = 0.5 * (v_ext[:, 1:-1, :-1] + v_ext[:, 1:-1, 1:])
    flux_vv = cen_v * cen_v
    flux_uv = side_u * side_v
    tend_v = -(flux_vv[:, 1:, :] - flux_vv[:, :-1, :] + flux_uv[:, :, 1:] - flux_uv[:, :, :-1] + p_ext[:, 2:, 1:-1] - p_ext[:, 1:-1, 1:-1]) / GRID_DX
    return tend_u, tend_v


def baroclinic_predict(vel_u, vel_v, value_a11, salinity, layout, halo_fn):
    n_levels = vel_u.shape[0]
    mask_c = level_mask(layout["k_cell"], n_levels)
    mask_u = level_mask(layout["k_u"], n_levels)
    mask_v = level_mask(layout["k_v"], n_levels)
    vel_um = vel_u * mask_u
    vel_vm = vel_v * mask_v
    density = mask_c * (BETA_S * (salinity - S_REF) - ALPHA_T * (value_a11 - T_REF))
    pressure = GRAVITY * layout["dz_cell"] * (jnp.cumsum(density, axis=0) - 0.5 * density)
    cell_coef = interface_coef(layout["k_cell"], layout["dz_cell"], DIFF_KT, n_levels)
    temp_mix = column_solve(value_a11 * mask_c, cell_coef)
    salt_mix = column_solve(salinity * mask_c, cell_coef)
    edges = halo_fn(jnp.stack([vel_um, vel_vm, pressure, temp_mix, salt_mix]))
    tend_u, tend_v = momentum_tend(edges[0], edges[1], edges[2])
    u_star = column_solve(mask_u * (vel_um + TIME_STEP * tend_u), interface_coef(layout["k_u"], layout["dz_u"], VISC_KV, n_levels))
    v_star = column_solve(mask_v * (vel_vm + TIME_STEP * tend_v), interface_coef(layout["k_v"], layout["dz_v"], VISC_KV, n_levels))
    forcing = jnp.stack([jnp.sum(layout["dz_u"] * (u_star - vel_um), axis=0), jnp.sum(layout["dz_v"] * (v_star - vel_vm), axis=0)]) / TIME_STEP
    return u_star, v_star, forcing, edges[3:], (mask_c, mask_u, mask_v)


def barotropic(eta_start, trans_start, face_depth, face_wet, wet_cell, forcing, tide_force, halo_fn):
    n_sub = tide_force.shape[0]
    dt_sub = TIME_STEP / n_sub
    weight_norm = 6.0 / (n_sub * (n_sub + 1) * (n_sub + 2))

    def substep(step, carry):
        eta_now, trans_now, trans_avg = carry
        trans_ext = halo_fn(trans_now)
        divergence = (trans_now[0] - trans_ext[0, 1:-1, :-2] + trans_now[1] - trans_ext[1, :-2, 1:-1]) / GRID_DX
        eta_next = wet_cell * (eta_now - dt_sub * divergence)
        eta_ext = halo_fn(eta_next)
        slope = jnp.stack([eta_ext[1:-1, 2:] - eta_next, eta_ext[2:, 1:-1] - eta_next]) / GRID_DX
        tide_now = lax.dynamic_index_in_dim(tide_force, step, 0, keepdims=False)
        trans_next = face_wet * (trans_now + dt_sub * (face_depth * (tide_now[:, None, None] - GRAVITY * slope) + forcing))
        weight = weight_norm * ((step + 1) * (n_sub - step)).astype(jnp.float32)
        return eta_next, trans_next, trans_avg + weight * trans_next

    return lax.fori_loop(0, n_sub, substep, (eta_start, trans_start, jnp.zeros_like(trans_start)))


def correct_velocity(star, dz_face, depth_face, mean_trans, mask):
    safe = jnp.where(depth_face > 0, depth_face, 1.0)
    return mask * (star + ((mean_trans - jnp.sum(dz_face * star, axis=0)) / safe)[None])


def advect_tracers(tracer_ext, flow_ext, mask_c):
    flux_x = flow_ext[0, :, 1:-1, :-1] * (0.5 * (tracer_ext[..., 1:-1, :-1] + tracer_ext[..., 1:-1, 1:]))
    flux_y = flow_ext[1, :, :-1, 1:-1] * (0.5 * (tracer_ext[..., :-1, 1:-1] + tracer_ext[..., 1:, 1:-1]))
    divergence = (flux_x[..., 1:] - flux_x[..., :-1] + flux_y[..., 1:, :] - flux_y[..., :-1, :]) / GRID_DX
    return mask_c * (tracer_ext[..., 1:-1, 1:-1] - TIME_STEP * divergence)


def baroclinic_finish(u_star, v_star, trans_avg, face_depth, layout, tracer_ext, masks, halo_fn):
    mask_c, mask_u, mask_v = masks
    vel_uc = correct_velocity(u_star, layout["dz_u"], face_depth[0], trans_avg[0], mask_u)
    vel_vc = correct_velocity(v_star, layout["dz_v"], face_depth[1], trans_avg[1], mask_v)
    flows = halo_fn(jnp.stack([vel_uc, vel_vc]))
    tracers = advect_tracers(tracer_ext, flows, mask_c)
    return vel_uc, vel_vc, tracers[0], tracers[1]


def ocean_step(vel_u, vel_v, value_a11, salinity, sea_level, trans_u, trans_v, bathymetry, kmt_levels, tide_force, halo_fn):
    layout = geometry(halo_fn(kmt_levels), halo_fn(bathymetry))
    u_star, v_star, forcing, tracer_ext, masks = baroclinic_predict(vel_u, vel_v, value_a11, salinity, layout, halo_fn)
    face_depth, face_wet, wet_cell = surface_fields(layout)
    eta_new, trans_new, trans_avg = barotropic(wet_cell * sea_level, face_wet * jnp.stack([trans_u, trans_v]), face_depth, face_wet, wet_cell, forcing, tide_force, halo_fn)
    vel_uc, vel_vc, temp_new, salt_new = baroclinic_finish(u_star, v_star, trans_avg, face_depth, layout, tracer_ext, masks, halo_fn)
    return eta_new, trans_new[0], trans_new[1], vel_uc, vel_vc, temp_new, salt_new


def solution(mesh):
    n_cols = mesh.shape["col"]
    n_rows = mesh.shape["row"]
    east_perm = [(member, (member - 1) % n_cols) for member in range(n_cols)]
    west_perm = [(member, (member + 1) % n_cols) for member in range(n_cols)]
    north_perm = [(member, member - 1) for member in range(1, n_rows)]
    south_perm = [(member, member + 1) for member in range(n_rows - 1)]

    def halo_swap(field):
        from_east = lax.ppermute(field[..., :1], "col", east_perm)
        from_west = lax.ppermute(field[..., -1:], "col", west_perm)
        wide = jnp.concatenate([from_west, field, from_east], axis=-1)
        from_north = lax.ppermute(wide[..., :1, :], "row", north_perm)
        from_south = lax.ppermute(wide[..., -1:, :], "row", south_perm)
        return jnp.concatenate([from_south, wide, from_north], axis=-2)

    def local_step(vel_u, vel_v, value_a11, salinity, sea_level, trans_u, trans_v, bathymetry, kmt_levels, tide_force):
        return ocean_step(vel_u, vel_v, value_a11, salinity, sea_level, trans_u, trans_v, bathymetry, kmt_levels, tide_force, halo_swap)

    spec_cube = P(None, "row", "col")
    spec_plane = P("row", "col")
    return jax.shard_map(local_step, mesh=mesh, in_specs=(spec_cube, spec_cube, spec_cube, spec_cube, spec_plane, spec_plane, spec_plane, spec_plane, spec_plane, P(None, None)), out_specs=(spec_plane, spec_plane, spec_plane, spec_cube, spec_cube, spec_cube, spec_cube), check_vma=False)
```

profile of v0, /device:TPU:0, one launch (start us, length us, event | category | flops | bytes accessed | tf_op | source)
XLA Modules:
  0.0 2665.2 jit_solution(14286799390366161898)
XLA Ops:
  10.0 21.9 fusion.61
  64.0 17.3 fusion.99
  97.5 91.0 %while.156 = (s32[]{:T(128)}, f32[256,512]{1,0:T(8,128)S(1)}, f32[256,512]{1,0:T(8,128)S(1)}, f32[31,256,512]{2,1,0:T(8,128)}, f32[31,256,512]{2,1,0:T(8,128)}, ...) while((s32[]{:T(128)}, f32[256,512]{1,0:T(8,128)S(1)}, ...), condition=%wide.region_6.7_spmd.clone, body=%wide.region_5.6_spmd.clone.sunk | while | flops 1048579 | bytes 5243511 | solution.py:44
  196.1 76.5 %while.157 = (s32[]{:T(128)}, f32[256,512]{1,0:T(8,128)S(1)}, f32[31,256,512]{2,1,0:T(8,128)}, f32[31,256,512]{2,1,0:T(8,128)}, f32[31,256,512]{2,1,0:T(8,128)}, /*index=5*/s32[]{:T(128)}, s32[]{:T(128)}, s32[]{:T(128)}) while((s32[]{:T(128)}, f32[256,512]{1,0:T(8,128)S(1)}, f32[31,256,512]{2,1,0:T(8,128)}, ...), condition=%wide.region_8.9_spmd.clone, body=%wide.region_7.8_spmd.clone.sunk | while | flops 393220 | bytes 2621551 | solution.py:51
  288.7 90.9 %while.154 = (s32[]{:T(128)}, f32[256,512]{1,0:T(8,128)S(1)}, f32[256,512]{1,0:T(8,128)S(1)}, f32[31,256,512]{2,1,0:T(8,128)}, f32[31,256,512]{2,1,0:T(8,128)}, ...) while((s32[]{:T(128)}, f32[256,512]{1,0:T(8,128)S(1)}, ...), condition=%wide.region_2.3_spmd.clone, body=%wide.region_1.2_spmd.clone.sunk | while | flops 1048579 | bytes 5243511 | solution.py:44
  387.4 76.7 %while.155 = (s32[]{:T(128)}, f32[256,512]{1,0:T(8,128)S(1)}, f32[31,256,512]{2,1,0:T(8,128)}, f32[31,256,512]{2,1,0:T(8,128)}, f32[31,256,512]{2,1,0:T(8,128)}, /*index=5*/s32[]{:T(128)}, s32[]{:T(128)}, s32[]{:T(128)}) while((s32[]{:T(128)}, f32[256,512]{1,0:T(8,128)S(1)}, f32[31,256,512]{2,1,0:T(8,128)}, ...), condition=%wide.region_4.5_spmd.clone, body=%wide.region_3.4_spmd.clone.sunk | while | flops 393220 | bytes 2621551 | solution.py:51
  491.0 19.1 bitcast_dynamic-update-slice_fusion.12
  533.8 29.4 %fusion.97 = (f32[5,31,256,1]{3,2,1,0:T(8,128)}, f32[5,31,256,1]{3,2,1,0:T(8,128)}) fusion(f32[5,31,256,512]{3,2,1,0:T(8,128)} %constant_dynamic-update-slice_fusion), kind=kLoop, calls=%fused_computation.228 | loop fusion | bytes 634880 | tf_op jit(solution)/shard_map/slice | solution.py:166
  589.9 28.9 %fusion.98 = (f32[31,256,512]{2,1,0:T(8,128)}, f32[31,256,512]{2,1,0:T(8,128)}, f32[31,256,512]{2,1,0:T(8,128)}) fusion(f32[30,256,512]{2,1,0:T(8,128)} %get-tuple-element.1252), kind=kLoop, calls=%fused_computation.229 | loop fusion | flops 8126464 | bytes 64487424 | tf_op jit(solution)/shard_map/concatenate | solution.py:32
  618.9 17.4 fusion.100
  673.4 55.9 %maximum_bitcast_fusion.1 = (f32[31,258,514]{2,1,0:T(8,128)}, f32[31,258,514]{2,1,0:T(8,128)}, f32[31,258,514]{2,1,0:T(8,128)}) fusion(f32[5,31,1,514]{3,2,1,0:T(1,128)S(1)} %collective-permute-done.17, f32[5,31,1,514]{3,2,1,0:T(1,128)S(1)} %collective-permute-done.16, f32[5,31,256,1]{3,2,1,0:T(8,128)} %copy.21, ...), kind=kLoop, calls=%fused_computation.99 | loop fusion | flops 49331664 | bytes 131551104 | tf_op jit(solution)/shard_map/squeeze | solution.py:99
  729.4 50.1 %fusion.42 = (f32[31,256,513]{2,1,0:T(8,128)}, f32[31,256,513]{2,1,0:T(8,128)}) fusion(f32[31,258,514]{2,1,0:T(8,128)} %get-tuple-element.1206, f32[31,258,514]{2,1,0:T(8,128)} %get-tuple-element.1207), kind=kLoop, calls=%fused_computation.111 | loop fusion | flops 32569344 | bytes 113992704 | tf_op jit(solution)/shard_map/mul | solution.py:74
  779.5 47.5 %fusion.48 = (f32[31,257,512]{2,1,0:T(8,128)}, f32[31,257,512]{2,1,0:T(8,128)}) fusion(f32[31,258,514]{2,1,0:T(8,128)} %get-tuple-element.1206, f32[31,258,514]{2,1,0:T(8,128)} %get-tuple-element.1207), kind=kLoop, calls=%fused_computation.123 | loop fusion | flops 32632832 | bytes 114214912 | tf_op jit(solution)/shard_map/mul | solution.py:75
  827.0 83.8 %fusion.59 = (f32[31,256,512]{2,1,0:T(8,128)}, f32[31,256,512]{2,1,0:T(8,128)}) fusion(f32[31,258,514]{2,1,0:T(8,128)} %get-tuple-element.1208, f32[31,257,512]{2,1,0:T(8,128)} %get-tuple-element.1221, f32[31,256,513]{2,1,0:T(8,128)} %get-tuple-element.1219, f32[31,256,512]{2,1,0:T(8,128)} %param.28, s32[256,512]{1,0:T(8,128)S(1)} %copy-done.9, ...), kind=kLoop, calls=%fused_computation.142 | loop fusion | flops 89391104 | bytes 244842496 | tf_op jit(solution)/shard_map/mul | solution.py:100
  926.7 90.9 %while.158 = (s32[]{:T(128)}, f32[256,512]{1,0:T(8,128)S(1)}, f32[256,512]{1,0:T(8,128)S(1)}, f32[31,256,512]{2,1,0:T(8,128)}, f32[31,256,512]{2,1,0:T(8,128)}, ...) while((s32[]{:T(128)}, f32[256,512]{1,0:T(8,128)S(1)}, ...), condition=%wide.region_10.11_spmd.clone, body=%wide.region_9.10_spmd.clone.sunk | while | flops 1048579 | bytes 5243511 | solution.py:44
  1025.3 76.5 %while.159 = (s32[]{:T(128)}, f32[256,512]{1,0:T(8,128)S(1)}, f32[31,256,512]{2,1,0:T(8,128)}, f32[31,256,512]{2,1,0:T(8,128)}, f32[31,256,512]{2,1,0:T(8,128)}, /*index=5*/s32[]{:T(128)}, s32[]{:T(128)}, s32[]{:T(128)}) while((s32[]{:T(128)}, f32[256,512]{1,0:T(8,128)S(1)}, f32[31,256,512]{2,1,0:T(8,128)}, ...), condition=%wide.region_12.13_spmd.clone, body=%wide.region_11.12_spmd.clone.sunk | while | flops 393220 | bytes 2621551 | solution.py:51
  1130.6 90.9 %while.160 = (s32[]{:T(128)}, f32[256,512]{1,0:T(8,128)S(1)}, f32[256,512]{1,0:T(8,128)S(1)}, f32[31,256,512]{2,1,0:T(8,128)}, f32[31,256,512]{2,1,0:T(8,128)}, ...) while((s32[]{:T(128)}, f32[256,512]{1,0:T(8,128)S(1)}, ...), condition=%wide.region_15.16_spmd.clone, body=%wide.region_14.15_spmd.clone.sunk | while | flops 1048579 | bytes 5243511 | solution.py:44
  1229.6 76.3 %while.161 = (s32[]{:T(128)}, f32[256,512]{1,0:T(8,128)S(1)}, f32[31,256,512]{2,1,0:T(8,128)}, f32[31,256,512]{2,1,0:T(8,128)}, f32[31,256,512]{2,1,0:T(8,128)}, /*index=5*/s32[]{:T(128)}, s32[]{:T(128)}, s32[]{:T(128)}) while((s32[]{:T(128)}, f32[256,512]{1,0:T(8,128)S(1)}, f32[31,256,512]{2,1,0:T(8,128)}, ...), condition=%wide.region_17.18_spmd.clone, body=%wide.region_16.17_spmd.clone.sunk | while | flops 393220 | bytes 2621551 | solution.py:51
  1320.6 1071.9 %while.162 = (s32[]{:T(128)}, f32[256,512]{1,0:T(8,128)S(1)}, f32[2,256,512]{2,1,0:T(8,128)S(1)}, f32[2,256,512]{2,1,0:T(8,128)}, f32[256,512]{1,0:T(8,128)}, /*...) while((s32[]{:T(128)}, f32[256,512]{1,0:T(8,128)S(1)}, ...), condition=%wide.region_20.21_spmd.clone, body=%wide.region_19.20_spmd.clone.sunk | while | flops 4721683 | bytes 15812171 | solution.py:123
  2394.6 17.1 add_select_fusion
  2474.2 43.5 %fusion.29 = f32[2,31,256,513]{3,2,1,0:T(8,128)} fusion(f32[5,31,256,1]{3,2,1,0:T(8,128)} %copy.21, f32[5,31,256,512]{3,2,1,0:T(8,128)} %constant_dynamic-update-slice_fusion, f32[5,31,256,1]{3,2,1,0:T(8,128)S(1)} %bitcast.257, f32[31,256,513]{2,1,0:T(8,128)} %fusion.37), kind=kLoop, calls=%fused_computation.77 | loop fusion | flops 32569344 | bytes 130436096 | tf_op jit(solution)/shard_map/mul | solution.py:132
  2531.1 42.2 %fusion.31 = f32[2,31,257,512]{3,2,1,0:T(8,128)} fusion(f32[5,31,1,514]{3,2,1,0:T(1,128)S(1)} %copy-done.34, f32[5,31,256,1]{3,2,1,0:T(8,128)} %copy.21, f32[5,31,256,512]{3,2,1,0:T(8,128)} %constant_dynamic-update-slice_fusion, f32[5,31,256,1]{3,2,1,0:T(8,128)} %copy.20, f32[5,31,1,514]{3,2,1,0:T(1,128)S(1)} %copy-done.32, f32[31,257,512]{2,1,0:T(8,128)} %fusion.44), kind=kLoop, calls=%fused_computation.81 | loop fusion | flops 65265664 | bytes 131168688 | tf_op jit(solution)/shard_map/mul | solution.py:133
  2573.4 69.9 %fusion.34 = f32[2,31,256,512]{3,2,1,0:T(8,128)} fusion(f32[2,31,257,512]{3,2,1,0:T(8,128)} %fusion.31, f32[2,31,256,513]{3,2,1,0:T(8,128)} %fusion.29, f32[1,31,256,512]{3,2,1,0:T(8,128)} %bitcast.268, f32[1,31,256,512]{3,2,1,0:T(8,128)} %bitcast.269, f32[31,256,512]{2,1,0:T(8,128)} %fusion.60), kind=kLoop, calls=%fused_computation.90 | loop fusion | flops 56885248 | bytes 211288064 | tf_op jit(solution)/shard_map/mul | solution.py:135
  2643.2 21.7 slice_bitcast_fusion
  (1047 shorter events, 2096.3 us)
Async XLA Ops:
  1.7 38.1 %collective-permute-start.6 = (s32[256,1]{1,0:T(8,128)S(1)}, s32[256,1]{1,0:T(8,128)S(1)}, u32[]{:S(2)}, u32[]{:S(2)}) collective-permute-start(s32[256,1]{1,0:T(8,128)S(1)} %get-tuple-element.1249), channel_id=1, source_target_pairs={{0,6},{2,0},{4,2},{6,4},{1,7},{3,1},{5,3},{7,5}} | collective-permute-start | bytes 3080 | tf_op jit(solution)/shard_map/ppermute | solution.py:165
  6.0 33.7 %collective-permute-start.7 = (s32[256,1]{1,0:T(8,128)S(1)}, s32[256,1]{1,0:T(8,128)S(1)}, u32[]{:S(2)}, u32[]{:S(2)}) collective-permute-start(s32[256,1]{1,0:T(8,128)S(1)} %get-tuple-element.1248), channel_id=1, source_target_pairs={{0,2},{2,4},{4,6},{6,0},{1,3},{3,5},{5,7},{7,1}} | collective-permute-start | bytes 3080 | tf_op jit(solution)/shard_map/ppermute | solution.py:166
  7.1 37.1 %collective-permute-start.10 = (f32[256,1]{1,0:T(8,128)S(1)}, f32[256,1]{1,0:T(8,128)S(1)}, u32[]{:S(2)}, u32[]{:S(2)}) collective-permute-start(f32[256,1]{1,0:T(8,128)S(1)} %get-tuple-element.1251), channel_id=1, source_target_pairs={{0,6},{2,0},{4,2},{6,4},{1,7},{3,1},{5,3},{7,5}} | collective-permute-start | bytes 3080 | tf_op jit(solution)/shard_map/ppermute | solution.py:165
  10.0 34.1 %collective-permute-start.9 = (f32[256,1]{1,0:T(8,128)S(1)}, f32[256,1]{1,0:T(8,128)S(1)}, u32[]{:S(2)}, u32[]{:S(2)}) collective-permute-start(f32[256,1]{1,0:T(8,128)S(1)} %get-tuple-element.1250), channel_id=1, source_target_pairs={{0,2},{2,4},{4,6},{6,0},{1,3},{3,5},{5,7},{7,1}} | collective-permute-start | bytes 3080 | tf_op jit(solution)/shard_map/ppermute | solution.py:166
  575.0 65.7 %collective-permute-start.14 = (f32[5,31,256,1]{2,3,1,0:T(1,128)}, f32[5,31,256,1]{2,3,1,0:T(1,128)}, u32[]{:S(2)}, u32[]{:S(2)}) collective-permute-start(f32[5,31,256,1]{2,3,1,0:T(1,128)} %copy.18), channel_id=1, source_target_pairs={{0,2},{2,4},{4,6},{6,0},{1,3},{3,5},{5,7},{7,1}} | collective-permute-start | bytes 476168 | tf_op jit(solution)/shard_map/ppermute | solution.py:166
  588.9 62.3 %collective-permute-start.15 = (f32[5,31,256,1]{2,3,1,0:T(1,128)}, f32[5,31,256,1]{2,3,1,0:T(1,128)}, u32[]{:S(2)}, u32[]{:S(2)}) collective-permute-start(f32[5,31,256,1]{2,3,1,0:T(1,128)} %copy.19), channel_id=1, source_target_pairs={{0,6},{2,0},{4,2},{6,4},{1,7},{3,1},{5,3},{7,5}} | collective-permute-start | bytes 476168 | tf_op jit(solution)/shard_map/ppermute | solution.py:165
  1500.2 14.2 collective-permute-start.1
  1535.9 14.2 collective-permute-start.1
  1571.6 14.2 collective-permute-start.1
  1607.3 14.2 collective-permute-start.1
  1643.0 14.2 collective-permute-start.1
  1678.7 14.2 collective-permute-start.1
  1714.4 14.2 collective-permute-start.1
  1750.1 14.2 collective-permute-start.1
  1785.8 14.2 collective-permute-start.1
  1892.9 14.2 collective-permute-start.1
  2000.0 14.2 collective-permute-start.1
  2035.7 14.2 collective-permute-start.1
  2107.1 14.2 collective-permute-start.1
  2142.8 14.2 collective-permute-start.1
  2249.9 14.2 collective-permute-start.1
  2357.0 14.2 collective-permute-start.1
  2436.8 25.4 collective-permute-start.19
  2469.9 47.8 %collective-permute-start.20 = (f32[2,31,1,514]{3,2,1,0:T(1,128)S(1)}, f32[2,31,1,514]{3,2,1,0:T(1,128)S(1)}, u32[]{:S(2)}, u32[]{:S(2)}) collective-permute-start(f32[2,31,1,514]{3,2,1,0:T(1,128)S(1)} %pad_maximum_fusion.35), channel_id=1, source_target_pairs={{0,1},{2,3},{4,5},{6,7}} | collective-permute-start | bytes 382424 | tf_op jit(solution)/shard_map/ppermute | solution.py:169
  (223 other events, 2488.6 us)
where the time goes:
time: 2680 us; the launch traced here: 2670 us
  other arithmetic  1500 us (56%)
  waiting for transfers between devices  653 us (24%)
  local copies, waits for them, and re-layouts  287 us (11%)
  starting transfers between devices  225 us (8%)
    dynamic_update_slice x248, other arithmetic, column_solve(): _, (gains, parts) = lax.scan(forward, start, (lower, diag, upper, source))  669 us
    ppermute x64, waiting for transfers between devices, halo_swap(): from_east = lax.ppermute(field[..., :1], 'col', east_perm)  345 us
    ppermute x64, waiting for transfers between devices, halo_swap(): from_west = lax.ppermute(field[..., -1:], 'col', west_perm)  251 us
    add x30, other arithmetic, substep(): return (eta_next, trans_next, trans_avg + weight * trans_next)  117 us
    ppermute x64, starting transfers between devices, halo_swap(): from_west = lax.ppermute(field[..., -1:], 'col', west_perm)  109 us
    another operation x12, local copies, waits for them, and re-layouts  95.4 us
    mul x1, other arithmetic, baroclinic_predict(): mask_u * (vel_um + TIME_STEP * tend_u)  83.8 us
    slice x65, local copies, waits for them, and re-layouts, halo_swap(): from_west = lax.ppermute(field[..., -1:], 'col', west_perm)  73 us
  transfers between devices with their start and end apart: 195, of which 181 were waited for; matrix products, arithmetic and copies ran while one was open for 7% of the time, Pallas kernels for 0%

commit v1 on v0

v1 whole, which is shorter than its diff:
```python
import functools

import jax
import jax.numpy as jnp
from jax import lax
from jax.experimental import pallas as pl
from jax.experimental.pallas import tpu as pltpu
from jax.sharding import PartitionSpec as P

MESH = pl.DeviceIdType.MESH
F32 = jnp.float32

TIME_STEP = 4.0
ALPHA_T = 0.02
BETA_S = 0.015
T_REF = 1.0
S_REF = 1.0
VISC_KV = 0.001
DIFF_KT = 0.0005

LANE = 128
LAST = LANE - 1
PAIR = 64
TAIL = 96
TILE = 8
STRIP = 32
MID = 40
ZERO = 0.0

NK = 31
NR = 256
NX = 512
NP = 4
RB = 32
NB = NR // RB
HALO = 32
ER = NR + HALO
VMEM_LIMIT = 62 * 1024 * 1024

ANY = pl.BlockSpec(memory_space=pl.ANY)
WHOLE = pl.BlockSpec(memory_space=pltpu.VMEM)


def lanes_of(shape):
    return lax.broadcasted_iota(jnp.int32, shape, len(shape) - 1)


def roll_to(x, source, target):
    return pltpu.roll(x, lax.rem(target - source + 256, LANE), x.ndim - 1)


def shift_east(planes):
    lane = lanes_of(planes[0].shape)
    rolled = [pltpu.roll(x, LAST, x.ndim - 1) for x in planes]
    return [jnp.where(lane == LAST, rolled[(n + 1) % len(planes)], rolled[n]) for n in range(len(planes))]


def shift_west(planes):
    lane = lanes_of(planes[0].shape)
    rolled = [pltpu.roll(x, 1, x.ndim - 1) for x in planes]
    return [jnp.where(lane == 0, rolled[n - 1], rolled[n]) for n in range(len(planes))]


def mix_kernel(t_ref, s_ref, uw_ref, ue_ref, vw_ref, ve_ref, kmt_ref, h_ref, eta_ref, tu_ref, tv_ref,
               p_out, t_out, s_out, ewa_out, eea_out, ewb_out, eeb_out, p1w_out, p1e_out,
               gain_s, pt_s, ps_s):

    def group(g, _):
        rows = pl.ds(pl.multiple_of(TILE * g, TILE), TILE)
        kf = kmt_ref[rows, :].astype(F32)
        dz = h_ref[rows, :] / jnp.maximum(kf, 1.0)
        safe = jnp.where(kf > 0, dz, 1.0)
        coef = (TIME_STEP * DIFF_KT) / (safe * safe)
        dz4 = 4.0 * dz
        zero = jnp.zeros_like(dz)
        cum, gain, pt, ps, low = zero, zero, zero, zero, zero
        for k in range(NK):
            wet = kf > k
            t = t_ref[k, rows, :]
            s = s_ref[k, rows, :]
            dens = jnp.where(wet, BETA_S * (s - S_REF) - ALPHA_T * (t - T_REF), ZERO)
            cum = cum + dens
            p4 = dz4 * (cum - 0.5 * dens)
            for l in range(NP):
                p_out[k, l, rows, :] = p4[:, LANE * l:LANE * l + LANE]
            up = jnp.where(kf > k + 1, coef, ZERO) if k < NK - 1 else zero
            inv = 1.0 / ((1.0 + up + low) - low * gain)
            gain = up * inv
            pt = (jnp.where(wet, t, ZERO) + low * pt) * inv
            ps = (jnp.where(wet, s, ZERO) + low * ps) * inv
            gain_s[k] = gain
            pt_s[k] = pt
            ps_s[k] = ps
            low = up
        bt, bs = zero, zero
        for k in range(NK - 1, -1, -1):
            gain = gain_s[k]
            bt = pt_s[k] + gain * bt
            bs = ps_s[k] + gain * bs
            for l in range(NP):
                t_out[k, l, rows, :] = bt[:, LANE * l:LANE * l + LANE]
                s_out[k, l, rows, :] = bs[:, LANE * l:LANE * l + LANE]
        return 0

    lax.fori_loop(0, RB // TILE, group, 0)

    lane = lanes_of((RB, LANE))

    def pack(k, carry):
        ewa, eea, ewb = carry
        for f, x in enumerate((uw_ref[k], vw_ref[k], p_out[k, 0], t_out[k, 0])):
            ewa = jnp.where(lane == STRIP * f + k, roll_to(x, 0, STRIP * f + k), ewa)
        for f, x in enumerate((ue_ref[k], ve_ref[k], t_out[k, 3], s_out[k, 3])):
            eea = jnp.where(lane == STRIP * f + k, roll_to(x, LAST, STRIP * f + k), eea)
        ewb = jnp.where(lane == STRIP + k, roll_to(s_out[k, 0], 0, STRIP + k), ewb)
        return ewa, eea, ewb

    zero = jnp.zeros((RB, LANE), F32)
    kf = kmt_ref[...].astype(F32)
    ewa, eea, ewb = lax.fori_loop(0, NK, pack, (zero, zero, zero))
    ewa_out[...] = ewa
    eea_out[...] = eea
    ewb_out[...] = jnp.where(lane < STRIP, kf[:, :LANE], ewb)
    eeb_out[...] = jnp.where(lane < STRIP, pltpu.roll(kf[:, 384:], STRIP, 1), ZERO)
    west, east = zero, zero
    for f, ref in enumerate((eta_ref, tu_ref, tv_ref, h_ref)):
        mine = (lane >= STRIP * f) & (lane < STRIP * f + STRIP)
        west = jnp.where(mine, pltpu.roll(ref[:, :LANE], STRIP * f, 1) if f else ref[:, :LANE], west)
        spun = (STRIP * f + STRIP) % LANE
        east = jnp.where(mine, pltpu.roll(ref[:, 384:], spun, 1) if spun else ref[:, 384:], east)
    p1w_out[...] = west
    p1e_out[...] = east


def mix(vel_u, vel_v, temp, salt, eta, trans_u, trans_v, depth, kmt):
    cube = pl.BlockSpec((NK, RB, NX), lambda r: (0, r, 0))
    west = pl.BlockSpec((NK, RB, LANE), lambda r: (0, r, 0))
    east = pl.BlockSpec((NK, RB, LANE), lambda r: (0, r, 3))
    plane = pl.BlockSpec((RB, NX), lambda r: (r, 0))
    out_cube = pl.BlockSpec((NK, NP, RB, LANE), lambda r: (0, 0, r, 0))
    edge = pl.BlockSpec((RB, LANE), lambda r: (r, 0))
    cubes = jax.ShapeDtypeStruct((NK, NP, NR, LANE), F32)
    edges = jax.ShapeDtypeStruct((NR, LANE), F32)
    return pl.pallas_call(
        mix_kernel,
        grid=(NB,),
        in_specs=[cube, cube, west, east, west, east, plane, plane, plane, plane, plane],
        out_specs=[out_cube] * 3 + [edge] * 6,
        out_shape=[cubes] * 3 + [edges] * 6,
        scratch_shapes=[pltpu.VMEM((NK, TILE, NX), F32)] * 3,
        compiler_params=pltpu.CompilerParams(vmem_limit_bytes=VMEM_LIMIT),
        name="mix",
    )(temp, salt, vel_u, vel_u, vel_v, vel_v, kmt, depth, eta, trans_u, trans_v)


def exchange_kernel(plan, n_cols, n_in, *refs):
    ins, outs = refs[:n_in], refs[n_in:-2]
    send_sem, recv_sem = refs[-2:]
    col, row = lax.axis_index("col"), lax.axis_index("row")
    west = lax.rem(col + n_cols - 1, n_cols)
    east = lax.rem(col + 1, n_cols)
    other = 1 - row
    peers = [(west, row), (east, row), (col, other), (west, other), (east, other)]
    barrier = pltpu.get_barrier_semaphore()
    for peer in peers:
        pl.semaphore_signal(barrier, inc=1, device_id=peer, device_id_type=MESH)
    pl.semaphore_wait(barrier, len(peers))

    copies = []

    def send(src, dst, peer):
        n = len(copies)
        copies.append(pltpu.make_async_remote_copy(
            src_ref=src, dst_ref=dst, send_sem=send_sem.at[n], recv_sem=recv_sem.at[n],
            device_id=peer, device_id_type=MESH))
        copies[-1].start()

    for kind, i, o, depth in plan:
        src, dst = ins[i], outs[o]
        start = pl.multiple_of((1 - row) * (NR - depth), TILE)
        if kind in ("west", "east"):
            to = west if kind == "west" else east
            send(src, dst.at[pl.ds(0, NR)], (to, row))
            if depth:
                send(src.at[pl.ds(start, depth)], dst.at[pl.ds(NR, depth)], (to, other))
        elif kind == "rows2":
            send(src.at[pl.ds(start, depth)], dst, (col, other))
        elif kind == "rows3":
            send(src.at[:, pl.ds(start, depth)], dst, (col, other))
        else:
            send(src.at[:, :, pl.ds(start, depth)], dst, (col, other))
    for copy in copies:
        copy.wait()


def exchange(n_cols, plan, ins, out_shapes, ident):
    n = sum(2 if kind in ("west", "east") and depth else 1 for kind, _, _, depth in plan)
    return pl.pallas_call(
        functools.partial(exchange_kernel, plan, n_cols, len(ins)),
        in_specs=[ANY] * len(ins),
        out_specs=[ANY] * len(out_shapes),
        out_shape=out_shapes,
        scratch_shapes=[pltpu.SemaphoreType.DMA((n,)), pltpu.SemaphoreType.DMA((n,))],
        compiler_params=pltpu.CompilerParams(collective_id=ident, has_side_effects=True),
        name=f"exchange{ident}",
    )(*ins)


def halo_tile(from_east, from_west, field):
    lane = lanes_of(from_east.shape)
    spun = (LANE - STRIP * field) % LANE
    e = pltpu.roll(from_east, spun, 1) if spun else from_east
    spun = (TAIL - STRIP * field) % LANE
    w = pltpu.roll(from_west, spun, 1) if spun else from_west
    return jnp.where(lane < STRIP, e, jnp.where(lane >= TAIL, w, ZERO))


def geometry_kernel(kmt_ref, h_ref, eta_ref, tu_ref, tv_ref, rep_ref, rwp_ref, reb_ref, rwb_ref,
                    rk_ref, rh_ref, reta_ref, rtu_ref, rtv_ref,
                    ku_out, kv_out, dzu_out, dzv_out, kc_out, eta_out, tu_out, tv_out, k_s, dz_s):
    row = lax.axis_index("row")

    def fill(c, _):
        rows = pl.ds(pl.multiple_of(RB * c, TILE), RB)

        def put(l, kf, h):
            k_s[l, rows, :] = kf
            dz_s[l, rows, :] = h / jnp.maximum(kf, 1.0)

        k_tile = halo_tile(reb_ref[rows, :], rwb_ref[rows, :], 0)
        h_tile = halo_tile(rep_ref[rows, :], rwp_ref[rows, :], 3)

        @pl.when(c < NB)
        def _():
            for l in range(NP):
                cut = slice(LANE * l, LANE * l + LANE)
                put(l, kmt_ref[rows, cut].astype(F32), h_ref[rows, cut])
                eta_out[l, rows, :] = eta_ref[rows, cut]
                tu_out[l, rows, :] = tu_ref[rows, cut]
                tv_out[l, rows, :] = tv_ref[rows, cut]

        @pl.when(c == NB)
        def _():
            for l in range(NP):
                cut = slice(LANE * l, LANE * l + LANE)
                put(l, rk_ref[:, cut].astype(F32), rh_ref[:, cut])
                eta_out[l, rows, :] = reta_ref[:, cut]
                tu_out[l, rows, :] = rtu_ref[:, cut]
                tv_out[l, rows, :] = rtv_ref[:, cut]

        put(NP, k_tile, h_tile)
        for f, out in enumerate((eta_out, tu_out, tv_out)):
            out[NP, rows, :] = halo_tile(rep_ref[rows, :], rwp_ref[rows, :], f)
        return 0

    lax.fori_loop(0, ER // RB, fill, 0)
    k_s[:, ER:ER + TILE, :] = k_s[:, 0:TILE, :]
    dz_s[:, ER:ER + TILE, :] = dz_s[:, 0:TILE, :]
    cut_row = jnp.where(row == 0, ER - 1, NR - 1)

    for c in range(ER // RB):
        base = RB * c
        rows = slice(base, base + RB)
        north = slice(base + 1, base + RB + 1)
        k = [k_s[l, rows, :] for l in range(NP + 1)]
        dz = [dz_s[l, rows, :] for l in range(NP + 1)]
        k_e = shift_east(k)
        dz_e = shift_east(dz)
        at = lax.broadcasted_iota(jnp.int32, (RB, LANE), 0) + base
        for l in range(NP + 1):
            ku = jnp.minimum(k[l], k_e[l])
            kv = jnp.where(at == cut_row, ZERO, jnp.minimum(k[l], k_s[l, north, :]))
            ku_out[l, rows, :] = ku
            kv_out[l, rows, :] = kv
            kc_out[l, rows, :] = k[l]
            dzu_out[l, rows, :] = 0.5 * (dz[l] + dz_e[l])
            dzv_out[l, rows, :] = 0.5 * (dz[l] + dz_s[l, north, :])
            eta_out[l, rows, :] = jnp.where(k[l] > 0, eta_out[l, rows, :], ZERO)
            tu_out[l, rows, :] = jnp.where(ku > 0, tu_out[l, rows, :], ZERO)
            tv_out[l, rows, :] = jnp.where(kv > 0, tv_out[l, rows, :], ZERO)


def geometry(*args):
    out = jax.ShapeDtypeStruct((NP + 1, ER, LANE), F32)
    return pl.pallas_call(
        geometry_kernel,
        in_specs=[WHOLE] * len(args),
        out_specs=[WHOLE] * TILE,
        out_shape=[out] * TILE,
        scratch_shapes=[pltpu.VMEM((NP + 1, ER + TILE, LANE), F32)] * 2,
        compiler_params=pltpu.CompilerParams(vmem_limit_bytes=VMEM_LIMIT),
        name="geometry",
    )(*args)


def window_copies(src, halo, buf, sem, r, slot, start):
    def piece(ref, lo, n, at, which):
        if len(ref.shape) == 4:
            pairs = [(ref.at[:, :, pl.ds(lo, n)], buf.at[slot, :, pl.ds(0, NP), pl.ds(at, n)])]
        else:
            pairs = [(ref.at[:, pl.ds(lo, n), pl.ds(LANE * l, LANE)], buf.at[slot, :, l, pl.ds(at, n)])
                     for l in range(NP)]
        for a, b in pairs:
            copy = pltpu.make_async_copy(a, b, sem.at[slot])
            if start:
                copy.start()
            else:
                copy.wait()

    piece(src, pl.multiple_of(RB * r, TILE), RB, TILE, 0)
    if start:
        @pl.when(r == 0)
        def _():
            piece(halo, 0, TILE, 0, 1)

        @pl.when(r > 0)
        def _():
            piece(src, pl.multiple_of(RB * r - TILE, TILE), TILE, 0, 1)

        @pl.when(r == NB - 1)
        def _():
            piece(halo, 0, TILE, RB + TILE, 2)

        @pl.when(r < NB - 1)
        def _():
            piece(src, pl.multiple_of(RB * r + RB, TILE), TILE, RB + TILE, 2)
    else:
        piece(halo, 0, TILE, 0, 1)
        piece(halo, 0, TILE, RB + TILE, 2)


def run_windows(r, slot, windows):
    @pl.when(r == 0)
    def _():
        for src, halo, buf, sem in windows:
            window_copies(src, halo, buf, sem, r, slot, True)

    @pl.when(r + 1 < NB)
    def _():
        for src, halo, buf, sem in windows:
            window_copies(src, halo, buf, sem, r + 1, 1 - slot, True)

    for src, halo, buf, sem in windows:
        window_copies(src, halo, buf, sem, r, slot, False)


def window_rows(r, ext_rows, far):
    prev = pl.multiple_of(jnp.where(r == 0, ext_rows - TILE, RB * r - TILE), TILE)
    main = pl.multiple_of(RB * r, TILE)
    nxt = pl.multiple_of(jnp.where(r == NB - 1, far, RB * r + RB), TILE)
    return (prev, TILE), (main, RB), (nxt, TILE)


def predict_kernel(u_hbm, v_hbm, p_hbm, ru_hbm, rv_hbm, rp_hbm, re_ref, rw_ref, ku_ref, kv_ref, dzu_ref, dzv_ref,
                   us_out, vs_out, fx_out, fy_out, su_out, sv_out, pw_out, pe_out,
                   ub, vb, pb, kw, ew, q_s, z_s, rhs_u, rhs_v, gu_s, pu_s, gv_s, pv_s, sem):
    r = pl.program_id(0)
    slot = lax.rem(r, 2)
    run_windows(r, slot, [(u_hbm, ru_hbm, ub, sem.at[0]), (v_hbm, rv_hbm, vb, sem.at[1]), (p_hbm, rp_hbm, pb, sem.at[2])])

    at = 0
    for lo, n in window_rows(r, ER, NR):
        for f, ref in enumerate((ku_ref, kv_ref)):
            kw[f, :, at:at + n, :] = ref[:, pl.ds(lo, n), :]
        at += n
    at = 0
    for lo, n in window_rows(r, NR + TILE, NR):
        for f, ref in enumerate((re_ref, rw_ref)):
            ew[f, at:at + n, :] = ref[pl.ds(lo, n), :]
        at += n

    lane48 = lanes_of((48, LANE))

    def tendency(k, _):
        kf = k.astype(F32)
        re, rw = ew[0], ew[1]
        for f, buf in enumerate((ub, vb)):
            for l in range(NP):
                buf[slot, k, l] = jnp.where(kw[f, l] > kf, buf[slot, k, l], ZERO)
            edge = jnp.where(lane48 == 0, roll_to(re, STRIP * f + k, 0), roll_to(rw, STRIP * f + k, LAST))
            buf[slot, k, NP] = jnp.where(kw[f, NP] > kf, edge, ZERO)
        pb[slot, k, NP] = roll_to(re, PAIR + k, 0)
        v0 = [vb[slot, k, l, 0:MID, :] for l in range(NP + 1)]
        v_e = shift_east(v0)
        for l in range(NP + 1):
            q_s[l, 0:MID, :] = (ub[slot, k, l, 0:MID, :] + ub[slot, k, l, 1:41, :]) * (v0[l] + v_e[l])
        for l in range(NP):
            c = vb[slot, k, l, TILE:48, :] + vb[slot, k, l, 7:47, :]
            z_s[l, TILE:48, :] = c * c + pb[slot, k, l, TILE:48, :]
        u0 = [ub[slot, k, l, TILE:MID, :] for l in range(NP + 1)]
        u_w = shift_west(u0)
        w = []
        for l in range(NP + 1):
            c = u0[l] + u_w[l]
            w.append(c * c + pb[slot, k, l, TILE:MID, :])
        w_e = shift_east(w)
        q0 = [q_s[l, TILE:MID, :] for l in range(NP + 1)]
        q_w = shift_west(q0)
        scale = TIME_STEP / 4.0
        for l in range(NP):
            tu = (w_e[l] - w[l]) + (q0[l] - q_s[l, 7:39, :])
            rhs_u[k, l] = jnp.where(kw[0, l, TILE:MID, :] > kf, u0[l] - scale * tu, ZERO)
            tv = (z_s[l, 9:41, :] - z_s[l, TILE:MID, :]) + (q0[l] - q_w[l])
            rhs_v[k, l] = jnp.where(kw[1, l, TILE:MID, :] > kf, vb[slot, k, l, TILE:MID, :] - scale * tv, ZERO)
        return 0

    lax.fori_loop(0, NK, tendency, 0)

    def solve(g, _):
        off = pl.multiple_of(TILE * g, TILE)
        rows = pl.ds(off, TILE)
        wrows = pl.ds(pl.multiple_of(TILE * g + TILE, TILE), TILE)
        grows = pl.ds(pl.multiple_of(RB * r + TILE * g, TILE), TILE)
        ku, kv = kw[0, 0:NP, wrows, :], kw[1, 0:NP, wrows, :]
        dzu, dzv = dzu_ref[0:NP, grows, :], dzv_ref[0:NP, grows, :]

        def coef_of(kf, dz):
            safe = jnp.where(kf > 0, dz, 1.0)
            return (TIME_STEP * VISC_KV) / (safe * safe)

        cu, cv = coef_of(ku, dzu), coef_of(kv, dzv)
        zero = jnp.zeros_like(cu)
        gu, pu, lu, gv, pv, lv = (zero,) * 6
        for k in range(NK):
            upu = jnp.where(ku > k + 1, cu, ZERO) if k < NK - 1 else zero
            upv = jnp.where(kv > k + 1, cv, ZERO) if k < NK - 1 else zero
            iu = 1.0 / ((1.0 + upu + lu) - lu * gu)
            iv = 1.0 / ((1.0 + upv + lv) - lv * gv)
            gu, gv = upu * iu, upv * iv
            pu = (rhs_u[k, :, rows, :] + lu * pu) * iu
            pv = (rhs_v[k, :, rows, :] + lv * pv) * iv
            gu_s[k], pu_s[k], gv_s[k], pv_s[k] = gu, pu, gv, pv
            lu, lv = upu, upv
        bu, bv, su, sv, du, dv = (zero,) * 6
        for k in range(NK - 1, -1, -1):
            bu = pu_s[k] + gu_s[k] * bu
            bv = pv_s[k] + gv_s[k] * bv
            us_out[k, :, rows, :] = bu
            vs_out[k, :, rows, :] = bv
            su = su + bu
            sv = sv + bv
            du = du + (bu - ub[slot, k, 0:NP, wrows, :])
            dv = dv + (bv - vb[slot, k, 0:NP, wrows, :])
        su_out[:, rows, :] = su
        sv_out[:, rows, :] = sv
        fx_out[:, rows, :] = dzu * du * (1.0 / TIME_STEP)
        fy_out[:, rows, :] = dzv * dv * (1.0 / TIME_STEP)
        return 0

    lax.fori_loop(0, RB // TILE, solve, 0)

    lane = lanes_of((RB, LANE))

    def pack(k, acc):
        return jnp.where(lane == PAIR + k, roll_to(us_out[k, NP - 1], LAST, PAIR + k), acc)

    acc = lax.fori_loop(0, NK, pack, jnp.zeros((RB, LANE), F32))
    pw_out[...] = jnp.where(lane < STRIP, fx_out[0], jnp.where(lane < PAIR, pltpu.roll(fy_out[0], STRIP, 1), ZERO))
    pe_out[...] = jnp.where(lane < STRIP, pltpu.roll(fx_out[NP - 1], STRIP, 1), jnp.where(lane < PAIR, pltpu.roll(fy_out[NP - 1], PAIR, 1), acc))


def predict(*args):
    out_cube = pl.BlockSpec((NK, NP, RB, LANE), lambda r: (0, 0, r, 0))
    out_plane = pl.BlockSpec((NP, RB, LANE), lambda r: (0, r, 0))
    edge = pl.BlockSpec((RB, LANE), lambda r: (r, 0))
    window = pltpu.VMEM((2, NK, NP + 1, RB + 16, LANE), F32)
    level = pltpu.VMEM((NP + 1, RB + 16, LANE), F32)
    return pl.pallas_call(
        predict_kernel,
        grid=(NB,),
        in_specs=[ANY] * 6 + [WHOLE] * 6,
        out_specs=[out_cube] * 2 + [out_plane] * 4 + [edge] * 2,
        out_shape=[jax.ShapeDtypeStruct((NK, NP, NR, LANE), F32)] * 2
        + [jax.ShapeDtypeStruct((NP, NR, LANE), F32)] * 4 + [jax.ShapeDtypeStruct((NR, LANE), F32)] * 2,
        scratch_shapes=[window] * 3 + [pltpu.VMEM((2, NP + 1, RB + 16, LANE), F32), pltpu.VMEM((2, RB + 16, LANE), F32), level, level]
        + [pltpu.VMEM((NK, NP, RB, LANE), F32)] * 2 + [pltpu.VMEM((NK, NP, TILE, LANE), F32)] * 4
        + [pltpu.SemaphoreType.DMA((3, 2))],
        compiler_params=pltpu.CompilerParams(vmem_limit_bytes=VMEM_LIMIT),
        name="predict",
    )(*args)


def barotropic_kernel(n_sub, tide_ref, ku_ref, kv_ref, dzu_ref, dzv_ref, kc_ref, eta_ref, tu_ref, tv_ref,
                      fx_ref, fy_ref, su_ref, sv_ref, ref_ref, rwf_ref, rfx_ref, rfy_ref, rvs_ref,
                      eta_out, tu_out, tv_out, cu_out, cv_out,
                      e_s, u_s, v_s, ub_s, vb_s, au_s, bu_s, av_s, bv_s, wet_s):
    dtb = TIME_STEP / n_sub
    weight_norm = 6.0 / (n_sub * (n_sub + 1) * (n_sub + 2))
    planes = range(NP + 1)

    def prepare(c, _):
        base = pl.multiple_of(RB * c, TILE)
        rows = pl.ds(base, RB)
        prow = pl.ds(base + TILE, RB)
        fe, fw = ref_ref[rows, :], rwf_ref[rows, :]

        def forces(l, fx, fy):
            ku, kv = ku_ref[l, rows, :], kv_ref[l, rows, :]
            wu = jnp.where(ku > 0, dtb, ZERO)
            wv = jnp.where(kv > 0, dtb, ZERO)
            au_s[l, rows, :] = wu * (ku * dzu_ref[l, rows, :])
            av_s[l, rows, :] = wv * (kv * dzv_ref[l, rows, :])
            bu_s[l, rows, :] = wu * fx
            bv_s[l, rows, :] = wv * fy

        @pl.when(c < NB)
        def _():
            for l in range(NP):
                forces(l, fx_ref[l, rows, :], fy_ref[l, rows, :])

        @pl.when(c == NB)
        def _():
            for l in range(NP):
                forces(l, rfx_ref[l], rfy_ref[l])

        forces(NP, halo_tile(fe, fw, 0), halo_tile(fe, fw, 1))
        for l in planes:
            wet_s[l, rows, :] = jnp.where(kc_ref[l, rows, :] > 0, dtb, ZERO)
            e_s[l, prow, :] = eta_ref[l, rows, :]
            u_s[l, rows, :] = tu_ref[l, rows, :]
            v_s[l, prow, :] = tv_ref[l, rows, :]
            ub_s[l, rows, :] = jnp.zeros((RB, LANE), F32)
            vb_s[l, rows, :] = jnp.zeros((RB, LANE), F32)
        return 0

    lax.fori_loop(0, ER // RB, prepare, 0)

    def substep(n, _):
        tx, ty = tide_ref[n, 0], tide_ref[n, 1]
        weight = weight_norm * ((n + 1) * (n_sub - n)).astype(F32)
        v_s[:, 0:TILE, :] = v_s[:, ER:ER + TILE, :]
        for c in range(ER // RB):
            b = RB * c
            u0 = [u_s[l, b:b + RB, :] for l in planes]
            u_w = shift_west(u0)
            for l in planes:
                div = (u0[l] - u_w[l]) + (v_s[l, b + TILE:b + TILE + RB, :] - v_s[l, b + 7:b + 7 + RB, :])
                e_s[l, b + TILE:b + TILE + RB, :] = e_s[l, b + TILE:b + TILE + RB, :] - wet_s[l, b:b + RB, :] * div
        e_s[:, ER + TILE:ER + 16, :] = e_s[:, TILE:16, :]
        for c in range(ER // RB):
            b = RB * c
            rows = slice(b, b + RB)
            prow = slice(b + TILE, b + TILE + RB)
            e0 = [e_s[l, prow, :] for l in planes]
            e_e = shift_east(e0)
            for l in planes:
                u = u_s[l, rows, :] + (au_s[l, rows, :] * (tx - (e_e[l] - e0[l])) + bu_s[l, rows, :])
                u_s[l, rows, :] = u
                ub_s[l, rows, :] = ub_s[l, rows, :] + weight * u
                v = v_s[l, prow, :] + (av_s[l, rows, :] * (ty - (e_s[l, b + 9:b + 9 + RB, :] - e0[l])) + bv_s[l, rows, :])
                v_s[l, prow, :] = v
                vb_s[l, rows, :] = vb_s[l, rows, :] + weight * v
        return 0

    lax.fori_loop(0, n_sub, substep, 0)

    def correction(mean, k, dz, total):
        depth = k * dz
        return (mean - dz * total) / jnp.where(depth > 0, depth, 1.0)

    def finish(c, _):
        base = pl.multiple_of(RB * c, TILE)
        rows = pl.ds(base, RB)
        prow = pl.ds(base + TILE, RB)
        for l in range(NP):
            cut = slice(LANE * l, LANE * l + LANE)
            eta_out[rows, cut] = e_s[l, prow, :]
            tu_out[rows, cut] = u_s[l, rows, :]
            tv_out[rows, cut] = v_s[l, prow, :]
            cu_out[l, rows, :] = correction(ub_s[l, rows, :], ku_ref[l, rows, :], dzu_ref[l, rows, :], su_ref[l, rows, :])
            cv_out[l, rows, :] = correction(vb_s[l, rows, :], kv_ref[l, rows, :], dzv_ref[l, rows, :], sv_ref[l, rows, :])
        fw = rwf_ref[rows, :]
        lane = lanes_of(fw.shape)
        total = jnp.sum(jnp.where((lane >= PAIR) & (lane < PAIR + NK), fw, ZERO), axis=1, keepdims=True)
        cu_out[NP, rows, :] = correction(ub_s[NP, rows, :], ku_ref[NP, rows, :], dzu_ref[NP, rows, :], total)
        return 0

    lax.fori_loop(0, NB, finish, 0)
    far = slice(ER - TILE, ER)
    for l in range(NP):
        total = rvs_ref[0, l]
        for k in range(1, NK):
            total = total + rvs_ref[k, l]
        cv_out[l, NR:NR + TILE, :] = correction(vb_s[l, far, :], kv_ref[l, far, :], dzv_ref[l, far, :], total)


def barotropic(tide, *args):
    n_sub = tide.shape[0]
    plane = jax.ShapeDtypeStruct((NR, NX), F32)
    scratch = [pltpu.VMEM((NP + 1, ER + 16, LANE), F32)] * 3 + [pltpu.VMEM((NP + 1, ER, LANE), F32)] * 7
    scratch[1] = pltpu.VMEM((NP + 1, ER, LANE), F32)
    return pl.pallas_call(
        functools.partial(barotropic_kernel, n_sub),
        in_specs=[pl.BlockSpec(memory_space=pltpu.SMEM)] + [WHOLE] * len(args),
        out_specs=[WHOLE] * 5,
        out_shape=[plane] * 3 + [jax.ShapeDtypeStruct((NP + 1, NR, LANE), F32), jax.ShapeDtypeStruct((NP, NR + TILE, LANE), F32)],
        scratch_shapes=scratch,
        compiler_params=pltpu.CompilerParams(vmem_limit_bytes=VMEM_LIMIT),
        name="barotropic",
    )(tide, *args)


def finish_kernel(us_ref, vs_hbm, t_hbm, s_hbm, rvs_hbm, rt_hbm, rs_hbm, rea_ref, rwa_ref, reb_ref, rwf_ref,
                  cu_ref, cv_ref, ku_ref, kv_ref, kc_ref,
                  u_out, v_out, t_out, s_out, vb, tb, sb, kvw, cvw, v_s, sem):
    r = pl.program_id(0)
    slot = lax.rem(r, 2)
    run_windows(r, slot, [(vs_hbm, rvs_hbm, vb, sem.at[0]), (t_hbm, rt_hbm, tb, sem.at[1]), (s_hbm, rs_hbm, sb, sem.at[2])])
    for (lo, n), (lo2, _), at in zip(window_rows(r, ER, NR)[:2], window_rows(r, NR + TILE, NR)[:2], (0, TILE)):
        kvw[:, at:at + n, :] = kv_ref[0:NP, pl.ds(lo, n), :]
        cvw[:, at:at + n, :] = cv_ref[:, pl.ds(lo2, n), :]
    main = pl.ds(pl.multiple_of(RB * r, TILE), RB)
    lane = lanes_of((RB, LANE))
    half = 0.5 * TIME_STEP

    def level(k, _):
        kf = k.astype(F32)
        u = []
        for l in range(NP):
            x = jnp.where(ku_ref[l, main, :] > kf, us_ref[k, l] + cu_ref[l, main, :], ZERO)
            u_out[k, :, LANE * l:LANE * l + LANE] = x
            u.append(half * x)
        x = roll_to(rwf_ref[main, :], PAIR + k, LAST)
        u.append(half * jnp.where(ku_ref[NP, main, :] > kf, x + cu_ref[NP, main, :], ZERO))
        for l in range(NP):
            x = jnp.where(kvw[l] > kf, vb[slot, k, l, 0:MID, :] + cvw[l], ZERO)
            v_out[k, :, LANE * l:LANE * l + LANE] = x[TILE:MID]
            v_s[l] = half * x
        rwa = rwa_ref[main, :]
        t_edge = jnp.where(lane == 0, roll_to(rea_ref[main, :], TAIL + k, 0), roll_to(rwa, PAIR + k, LAST))
        s_edge = jnp.where(lane == 0, roll_to(reb_ref[main, :], STRIP + k, 0), roll_to(rwa, TAIL + k, LAST))
        for buf, edge, out in ((tb, t_edge, t_out), (sb, s_edge, s_out)):
            x0 = [buf[slot, k, l, TILE:MID, :] for l in range(NP)] + [edge]
            x_e = shift_east(x0)
            fx = [u[l] * (x0[l] + x_e[l]) for l in range(NP + 1)]
            fx_w = shift_west(fx)
            for l in range(NP):
                fy = v_s[l, TILE:MID, :] * (x0[l] + buf[slot, k, l, 9:41, :])
                fy_s = v_s[l, 7:39, :] * (buf[slot, k, l, 7:39, :] + x0[l])
                new = x0[l] - ((fx[l] - fx_w[l]) + (fy - fy_s))
                out[k, :, LANE * l:LANE * l + LANE] = jnp.where(kc_ref[l, main, :] > kf, new, ZERO)
        return 0

    lax.fori_loop(0, NK, level, 0)


def finish(*args):
    cube = pl.BlockSpec((NK, NP, RB, LANE), lambda r: (0, 0, r, 0))
    out_cube = pl.BlockSpec((NK, RB, NX), lambda r: (0, r, 0))
    window = pltpu.VMEM((2, NK, NP, RB + 16, LANE), F32)
    return pl.pallas_call(
        finish_kernel,
        grid=(NB,),
        in_specs=[cube] + [ANY] * 6 + [WHOLE] * 9,
        out_specs=[out_cube] * 4,
        out_shape=[jax.ShapeDtypeStruct((NK, NR, NX), F32)] * 4,
        scratch_shapes=[window] * 3 + [pltpu.VMEM((NP, MID, LANE), F32)] * 3 + [pltpu.SemaphoreType.DMA((3, 2))],
        compiler_params=pltpu.CompilerParams(vmem_limit_bytes=VMEM_LIMIT),
        name="finish",
    )(*args)


def solution(mesh):
    n_cols = mesh.shape["col"]

    def shape(*dims, dtype=F32):
        return jax.ShapeDtypeStruct(dims, dtype)

    def local_step(vel_u, vel_v, temp, salt, eta, trans_u, trans_v, depth, kmt, tide):
        p4, t_mix, s_mix, ewa, eea, ewb, eeb, p1w, p1e = mix(vel_u, vel_v, temp, salt, eta, trans_u, trans_v, depth, kmt)
        plan = [("west", 0, 0, TILE), ("east", 1, 1, TILE), ("west", 2, 2, STRIP), ("east", 3, 3, STRIP), ("west", 4, 4, STRIP), ("east", 5, 5, STRIP)]
        plan += [("rows2", 6 + n, 6 + n, STRIP) for n in range(5)]
        plan += [("rows3", 11, 11, TILE), ("rows3", 12, 12, TILE)] + [("rows4", 13 + n, 13 + n, TILE) for n in range(3)]
        ins = [ewa, eea, ewb, eeb, p1w, p1e, kmt, depth, eta, trans_u, trans_v, vel_u, vel_v, p4, t_mix, s_mix]
        outs = [shape(NR + TILE, LANE)] * 2 + [shape(ER, LANE)] * 4 + [shape(HALO, NX, dtype=jnp.int32)] + [shape(HALO, NX)] * 4
        outs += [shape(NK, TILE, NX)] * 2 + [shape(NK, NP, TILE, LANE)] * 3
        rea, rwa, reb, rwb, rep, rwp, rk, rh, reta, rtu, rtv, ru, rv, rp, rt, rs = exchange(n_cols, plan, ins, outs, 0)
        ku, kv, dzu, dzv, kc, eta_x, tu_x, tv_x = geometry(kmt, depth, eta, trans_u, trans_v, rep, rwp, reb, rwb, rk, rh, reta, rtu, rtv)
        us, vs, fx, fy, su, sv, pw, pe = predict(vel_u, vel_v, p4, ru, rv, rp, rea, rwa, ku, kv, dzu, dzv)
        plan = [("west", 0, 0, STRIP), ("east", 1, 1, STRIP), ("rows3", 2, 2, STRIP), ("rows3", 3, 3, STRIP), ("rows4", 4, 4, TILE)]
        outs = [shape(ER, LANE)] * 2 + [shape(NP, HALO, LANE)] * 2 + [shape(NK, NP, TILE, LANE)]
        ref, rwf, rfx, rfy, rvs = exchange(n_cols, plan, [pw, pe, fx, fy, vs], outs, 1)
        eta_new, tu_new, tv_new, cu, cv = barotropic(tide, ku, kv, dzu, dzv, kc, eta_x, tu_x, tv_x, fx, fy, su, sv, ref, rwf, rfx, rfy, rvs)
        u_new, v_new, t_new, s_new = finish(us, vs, t_mix, s_mix, rvs, rt, rs, rea, rwa, reb, rwf, cu, cv, ku, kv, kc)
        return eta_new, tu_new, tv_new, u_new, v_new, t_new, s_new

    cube = P(None, "row", "col")
    plane = P("row", "col")
    return jax.shard_map(local_step, mesh=mesh, in_specs=(cube,) * 4 + (plane,) * 5 + (P(None, None),), out_specs=(plane,) * 3 + (cube,) * 4, check_vma=False)
```

time: 2680 us -> 308 us (0.11)
  other arithmetic: 1500 us -> 0 us
  waiting for transfers between devices: 653 us -> 0 us
  Pallas kernels: 0 us -> 306 us
  local copies, waits for them, and re-layouts: 287 us -> 1.37 us
  starting transfers between devices: 225 us -> 0 us
    dynamic_update_slice x248 -> x0, other arithmetic: 669 us -> none  [column_solve(): _, (gains, parts) = lax.scan(forward, start, (lower, diag, upper, source))]
    ppermute x195 -> x0, waiting for transfers between devices: 653 us -> none  [the longest x64 345 us: halo_swap(): from_east = lax.ppermute(field[..., :1], 'col', east_perm)]
    mul x44 -> x0, other arithmetic: 467 us -> none  [the longest x1 83.8 us: baroclinic_predict(): mask_u * (vel_um + TIME_STEP * tend_u)]
    pallas_call x0 -> x7, Pallas kernels: none -> 306 us  [the longest x1 115 us: predict(): pl.pallas_call(predict_kernel, grid=(NB,), in_specs=[ANY] * 6 + [WHOLE] *...]
    ppermute x195 -> x0, starting transfers between devices: 225 us -> none  [the longest x64 109 us: halo_swap(): from_west = lax.ppermute(field[..., -1:], 'col', west_perm)]
    add x32 -> x0, other arithmetic: 119 us -> none  [the longest x30 117 us: substep(): return (eta_next, trans_next, trans_avg + weight * trans_next)]
    another operation x13 -> x0, local copies, waits for them, and re-layouts: 107 us -> none
    slice x67 -> x0, local copies, waits for them, and re-layouts: 90.2 us -> none  [the longest x65 73 us: halo_swap(): from_west = lax.ppermute(field[..., -1:], 'col', west_perm)]
  transfers between devices with their start and end apart: 195 -> 0, of which waited for: 181 -> 0; matrix products, arithmetic and copies ran while one was open for 7% -> 0% of each run, Pallas kernels for 0% -> 0%
where the time goes in v1:
time: 308 us
  Pallas kernels  306 us (99%)
    pallas_call x1, Pallas kernels, predict(): pl.pallas_call(predict_kernel, grid=(NB,), in_specs=[ANY] * 6 + [WHOLE] *...  115 us
    pallas_call x1, Pallas kernels, finish(): pl.pallas_call(finish_kernel, grid=(NB,), in_specs=[cube] + [ANY] * 6 + [...  68.9 us
    pallas_call x1, Pallas kernels, mix(): pl.pallas_call(mix_kernel, grid=(NB,), in_specs=[cube, cube, west, east,...  52.9 us
    pallas_call x2, Pallas kernels, exchange(): pl.pallas_call(functools.partial(exchange_kernel, plan, n_cols, len(ins))...  35.2 us
    pallas_call x1, Pallas kernels, barotropic(): pl.pallas_call(functools.partial(barotropic_kernel, n_sub), in_specs=[pl....  27.6 us
    pallas_call x1, Pallas kernels, geometry(): pl.pallas_call(geometry_kernel, in_specs=[WHOLE] * len(args), out_specs=[...  6.44 us

profile of v1, /device:TPU:0, one launch (start us, length us, event | category | flops | bytes accessed | tf_op | source)
XLA Modules:
  0.0 307.8 jit_solution(7006483893244072249)
XLA Ops:
  0.6 1.4 copy.17.tide_ref
  2.0 52.9 %mix.1 = (f32[31,4,256,128]{3,2,1,0:T(8,128)}, f32[31,4,256,128]{3,2,1,0:T(8,128)}, f32[31,4,256,128]{3,2,1,0:T(8,128)}, f32[256,128]{1,0:T(8,128)}, f32[256,128...) custom-call(f32[31,256,512]{2,1,0:T(8,128)} %t_ref.1, ...), custom_call_target="tpu_custom_call" | custom-call | tf_op jit(solution)/shard_map/mix/pallas_call | solution.py:144
  54.9 24.8 %exchange0.1 = (f32[264,128]{1,0:T(8,128)}, f32[264,128]{1,0:T(8,128)}, f32[288,128]{1,0:T(8,128)}, f32[288,128]{1,0:T(8,128)}, f32[288,128]{1,0:T(8,128)}, /*in...) custom-call(f32[256,128]{1,0:T(8,128)} %get-tuple-element.62.refs_0_, ...), custom_call_target="tpu_custom_call" | custom-call | tf_op jit(solution)/shard_map/exchange0/pallas_call | solution.py:198
  79.7 6.4 %geometry.1 = (f32[5,288,128]{2,1,0:T(8,128)}, f32[5,288,128]{2,1,0:T(8,128)}, f32[5,288,128]{2,1,0:T(8,128)}, f32[5,288,128]{2,1,0:T(8,128)}, f32[5,288,128]{2,...) custom-call(s32[256,512]{1,0:T(8,128)} %kmt_ref.3, f32[256,512]{1,0:T(8,128)} %h_ref.3, ...), custom_call_target="tpu_custom_call" | custom-call | tf_op jit(solution)/shard_map/geometry/pallas_call | solution.py:285
  86.1 114.7 %predict.1 = (f32[31,4,256,128]{3,2,1,0:T(8,128)}, f32[31,4,256,128]{3,2,1,0:T(8,128)}, f32[4,256,128]{2,1,0:T(8,128)}, f32[4,256,128]{2,1,0:T(8,128)}, f32[4,25...) custom-call(f32[31,256,512]{2,1,0:T(8,128)} %u_hbm.1, ...), custom_call_target="tpu_custom_call" | custom-call | tf_op jit(solution)/shard_map/predict/pallas_call | solution.py:468
  200.9 10.4 %exchange1.1 = (f32[288,128]{1,0:T(8,128)}, f32[288,128]{1,0:T(8,128)}, f32[4,32,128]{2,1,0:T(8,128)}, f32[4,32,128]{2,1,0:T(8,128)}, f32[31,4,8,128]{3,2,1,0:T(8,128)}) custom-call(f32[256,128]{1,0:T(8,128)} %get-tuple-element.97.refs_0_, f32[256,128]{1,0:T(8,128)} %get-tuple-element.98.refs_1_, f32[4,256,128]{2,1,0:T(8,128)} %get-tuple-element.93.refs_2_.fx_ref, ...), custom_call_target="tpu_custom_call" | custom-call | tf_op jit(solution)/shard_map/exchange1/pallas_call | solution.py:198
  211.3 27.6 %barotropic.1 = (f32[256,512]{1,0:T(8,128)}, f32[256,512]{1,0:T(8,128)}, f32[256,512]{1,0:T(8,128)}, f32[5,256,128]{2,1,0:T(8,128)}, f32[4,264,128]{2,1,0:T(8,128)}) custom-call(f32[30,2]{1,0:T(8,128)} %copy.17.tide_ref, f32[5,288,128]{2,1,0:T(8,128)} %get-tuple-element.80.ku_ref, f32[5,288,128]{2,1,0:T(8,128)} %get-tuple-element.81.kv_ref, ...), custom_call_target="tpu_custom_call" | custom-call | tf_op jit(solution)/shard_map/barotropic/pallas_call | solution.py:592
  238.9 68.9 %finish.1 = (f32[31,256,512]{2,1,0:T(8,128)}, f32[31,256,512]{2,1,0:T(8,128)}, f32[31,256,512]{2,1,0:T(8,128)}, f32[31,256,512]{2,1,0:T(8,128)}) custom-call(f32[31,4,256,128]{3,2,1,0:T(8,128)} %get-tuple-element.108.us_ref, f32[31,4,256,128]{3,2,1,0:T(8,128)} %get-tuple-element.99.refs_4_.vs_hbm, f32[31,4,256,128]{3,2,1,0:T(8,128)} %get-tuple-element.69.refs_14_.t_hbm, ...), custom_call_target="tpu_custom_call" | custom-call | tf_op jit(solution)/shard_map/finish/pallas_call | solution.py:651
